TPU v7x, 128 devices: a whole 4x4x4 slice. The times are simulated.
128 devices in a mesh: section: 4 (over x), dp: 32 (over y, z, core).
Axes of the slice: x: 4, y: 4, z: 4, core: 2. Of those that a mesh axis runs over, the one named last changes fastest.
Arguments:
- clip_pool: bfloat16 [1024, 256, 512], P('dp'), may hold values from -8 to 8
- clip_index: int32 [8, 128], P(None, 'dp'), may hold values from 0 to 31, as said below
- batch_order: int32 [8], replicated, may hold values from 0 to 7, each once
- tap_weights: bfloat16 [4, 3, 512, 512], P('section'), may hold values from -0.15625 to 0.15625
- out_weights: bfloat16 [4, 512, 512], P('section'), may hold values from -0.25 to 0.25
- norm_gains: bfloat16 [4, 512], P('section'), may hold values from 0.099609375 to 1.8984375
- quant_weight: bfloat16 [512, 18], replicated, may hold values from -0.25 to 0.25
- quant_bias: float32 [18], replicated, may hold values from -3 to 3
- post_weight: bfloat16 [18, 512], replicated, may hold values from -1.5 to 1.5
Outputs:
- row_error: float32 [8, 128, 256], P('section', 'dp')
- entropy_loss: float32 [8], replicated
Inputs may be any that keep to these rules, and one draw needn't show every extreme that they name: `clip_index`: entries index the clips of the replica that holds the column; over all 8 micro-batches, the 4 columns of one replica name each of its 32 clips exactly once. `batch_order`: each micro-batch number 0 to 7 once.
All inputs are finite; a program needn't handle non-finite values.
Results may differ from a plain program's by a relative error of at most 0.0015.
Values may be sent and summed in bfloat16 or wider, within the bound.
A program may use at most 128 MiB of HBM per device.

v0:
```python
import functools
import jax
import jax.numpy as jnp
from jax import lax
from jax.sharding import Mesh
from jax.sharding import PartitionSpec as P

SPATIAL = 64
DP = ("dp_0", "dp_1", "dp_2")
SECTION_DP = ("section", "dp_0", "dp_1", "dp_2")
norm_eps = 1e-06
quant_section = 1


def over_axes(array, axes):
    return functools.reduce(lax.psum, axes, array)


def run_block(current, tap_set, out_weight, gain_row):
    clip_count, row_count, channels = current.shape
    widened = current.astype(jnp.float32)
    scale = lax.rsqrt(jnp.mean(widened * widened, axis=-1, keepdims=True) + norm_eps)
    normed = (widened * scale * gain_row.astype(jnp.float32)).astype(jnp.bfloat16)
    flat = normed.reshape(-1, channels)
    mixed = jnp.zeros((clip_count, row_count, channels), jnp.float32)
    for k in range(tap_set.shape[0]):
        product = jnp.dot(flat, tap_set[k], preferred_element_type=jnp.float32).reshape(
            clip_count, row_count, channels
        )
        moved = jnp.pad(product, ((0, 0), (k * SPATIAL, 0), (0, 0)))[:, :row_count]
        mixed = mixed + moved
    activated = jax.nn.silu(mixed).astype(jnp.bfloat16)
    update = jnp.dot(
        activated.reshape(-1, channels), out_weight, preferred_element_type=jnp.float32
    )
    return (widened + update.reshape(clip_count, row_count, channels)).astype(jnp.bfloat16)


def quantize(current, quant_weight, quant_bias, post_weight):
    channels = current.shape[-1]
    logits = (
        jnp.dot(current.reshape(-1, channels), quant_weight, preferred_element_type=jnp.float32)
        + quant_bias
    )
    bit_prob = jax.nn.sigmoid(4.0 * logits)
    codes = (2.0 * bit_prob - 1.0).astype(jnp.bfloat16)
    quantized = jnp.dot(codes, post_weight, preferred_element_type=jnp.float32).astype(jnp.bfloat16)
    bit_sums = jnp.sum(bit_prob, axis=0)
    entropy_sum = -jnp.sum(
        bit_prob * jax.nn.log_sigmoid(4.0 * logits)
        + (1.0 - bit_prob) * jax.nn.log_sigmoid(-4.0 * logits)
    )
    return (quantized.reshape(current.shape), bit_sums, entropy_sum)


def squared_error(decoded, source):
    differ = decoded.astype(jnp.float32) - source.astype(jnp.float32)
    return jnp.mean(differ * differ, axis=-1)


def final_entropy(bit_buffer, entropy_buffer, batch_order, rows_total):
    marginal = bit_buffer / rows_total
    sample_entropy = entropy_buffer / rows_total
    averaged = jnp.zeros_like(marginal)
    running = marginal[batch_order[0]]
    for t in range(batch_order.shape[0]):
        if t > 0:
            running = 0.5 * running + 0.5 * marginal[batch_order[t]]
        averaged = averaged.at[batch_order[t]].set(running)
    smoothed = 0.05 + 0.9 * averaged
    code_entropy = -jnp.sum(
        smoothed * jnp.log(smoothed) + (1.0 - smoothed) * jnp.log(1.0 - smoothed), axis=-1
    )
    return sample_entropy - code_entropy


def on_device(
    clip_pool,
    clip_index,
    batch_order,
    tap_weights,
    out_weights,
    norm_gains,
    quant_weight,
    quant_bias,
    post_weight,
):
    section_id = lax.axis_index("section")
    sections = lax.axis_size("section")
    batches = batch_order.shape[0]
    clip_count = clip_index.shape[1]
    row_count = clip_pool.shape[1]
    rows_total = float(clip_count * lax.axis_size(DP) * row_count)
    bit_buffer = jnp.zeros((batches, quant_weight.shape[1]), jnp.float32)
    entropy_buffer = jnp.zeros((batches,), jnp.float32)
    all_taps, all_out, all_gains = (
        lax.all_gather(tap_weights, "section", axis=0, tiled=True),
        lax.all_gather(out_weights, "section", axis=0, tiled=True),
        lax.all_gather(norm_gains, "section", axis=0, tiled=True),
    )
    per_section = batches // sections
    error_list = []
    for i in range(per_section):
        batch_slot = section_id * per_section + i
        source = jnp.take(clip_pool, clip_index[batch_slot], axis=0)
        current = source
        for s in range(sections):
            current = run_block(current, all_taps[s], all_out[s], all_gains[s])
            if s == quant_section:
                current, bit_sums, entropy_sum = quantize(
                    current, quant_weight, quant_bias, post_weight
                )
                bit_buffer = bit_buffer.at[batch_slot].add(bit_sums)
                entropy_buffer = entropy_buffer.at[batch_slot].add(entropy_sum)
        error_list.append(squared_error(current, source))
    bit_buffer, entropy_buffer = (
        over_axes(bit_buffer, SECTION_DP),
        over_axes(entropy_buffer, SECTION_DP),
    )
    error_out = jnp.stack(error_list)
    losses = final_entropy(bit_buffer, entropy_buffer, batch_order, rows_total)
    return (error_out, losses)


def solution(mesh):
    torus = Mesh(
        mesh.devices.reshape(mesh.shape["section"], 4, 4, 2), ("section", "dp_0", "dp_1", "dp_2")
    )
    return jax.shard_map(
        on_device,
        mesh=torus,
        in_specs=(
            P(DP, None, None),
            P(None, DP),
            P(),
            P("section", None, None, None),
            P("section", None, None),
            P("section", None),
            P(),
            P(),
            P(),
        ),
        out_specs=(P("section", DP, None), P()),
        check_vma=False,
    )
```

profile of v0, /device:TPU:1, one launch (start us, length us, event | category | flops | bytes accessed | tf_op | source)
XLA Modules:
  0.0 248.7 jit_solution(16837074438808056096)
XLA Ops:
  20.1 4.7 %gather_fusion = bf16[4,256,512]{2,1,0:T(8,128)(2,1)S(1)} fusion(bf16[32,256,512]{2,1,0:T(8,128)(2,1)} %param.35, s32[1024]{0:T(1024)S(1)} %pad_clamp_fusion.1), kind=kCustom, calls=%fused_computation.clone | custom fusion | bytes 2097168 | tf_op jit(solution)/shard_map/jit(_take)/gather | solution.py:105
  24.8 4.8 %gather_fusion.1 = bf16[4,256,512]{2,1,0:T(8,128)(2,1)S(1)} fusion(bf16[32,256,512]{2,1,0:T(8,128)(2,1)} %param.35, s32[1024]{0:T(1024)S(1)} %pad_clamp_fusion), kind=kCustom, calls=%fused_computation.1.clone | custom fusion | bytes 2097168 | tf_op jit(solution)/shard_map/jit(_take)/gather | solution.py:105
  34.9 10.8 %all-gather = bf16[4,1,512]{2,1,0:T(2,128)(2,1)S(1)} all-gather(bf16[1,1,512]{2,1,0:T(2,128)(2,1)S(1)} %bitcast.176), channel_id=1, replica_groups=mesh['section'=4,'dp_0'=4,'dp_1'=4,'dp_2'=2] {'section'}, dimensions={0}, use_global_device_ids=true | all-gather | bytes 5120 | tf_op jit(solution)/shard_map/all_gather | solution.py:99
  48.2 30.2 %all-gather.4.cloned.1.call-done = bf16[4,3,512,512]{3,2,1,0:T(8,128)(2,1)} async-done(((bf16[1,3,512,512]{3,2,1,0:T(8,128)(2,1)}), bf16[4,3,512,512]{3,2,1,0:T(8,128)(2,1)}) %all-gather.4.cloned.1.call-update) | async-done | bytes 6291472 | tf_op jit(solution)/shard_map/all_gather | solution.py:97
  84.8 26.6 %all-gather.6.cloned.1.call-done = bf16[4,512,512]{2,1,0:T(8,128)(2,1)} async-done(((bf16[1,512,512]{2,1,0:T(8,128)(2,1)}), bf16[4,512,512]{2,1,0:T(8,128)(2,1)}) %all-gather.6.cloned.1.call-update) | async-done | bytes 2097168 | tf_op jit(solution)/shard_map/all_gather | solution.py:98
  111.4 4.6 %fusion.24 = (f32[4,256]{1,0:T(4,128)S(1)}, bf16[4,256,512]{2,1,0:T(8,128)(2,1)}) fusion(bf16[4,512,512]{2,1,0:T(8,128)(2,1)} %all-gather.6.cloned.1.call-done, f32[4,256,512]{2,1,0:T(8,128)} %fusion.58, f32[4,256,512]{2,1,0:T(8,128)} %fusion.60, f32[4,256]{1,0:T(4,128)S(1)} %add_rsqrt_fusion.3, f32[512]{0:T(512)S(1)} %bitcast.191, ...), kind=kOutput, calls=%fused_computation.62 | convolution fusion | flops 1083702272 | bytes 8399872 | tf_op jit(solution)/shard_map/dot_general | solution.py:33
  116.1 3.5 %fusion.54 = f32[4,256,512]{2,1,0:T(8,128)} fusion(bf16[4,256,512]{2,1,0:T(8,128)(2,1)} %get-tuple-element.194, f32[4,256]{1,0:T(4,128)S(1)} %add_rsqrt_fusion.2, f32[512]{0:T(512)S(1)} %bitcast.183, bf16[4,3,512,512]{3,2,1,0:T(8,128)(2,1)} %all-gather.4.cloned.1.call-done), kind=kOutput, calls=%fused_computation.105 | convolution fusion | flops 538968064 | bytes 3676160 | tf_op jit(solution)/shard_map/dot_general | solution.py:27
  119.6 3.2 %fusion.52 = f32[4,256,512]{2,1,0:T(8,128)} fusion(bf16[4,256,512]{2,1,0:T(8,128)(2,1)S(1)} %copy-done.16, f32[4,256]{1,0:T(4,128)S(1)} %add_rsqrt_fusion.2, f32[512]{0:T(512)S(1)} %bitcast.184, bf16[4,3,512,512]{3,2,1,0:T(8,128)(2,1)} %all-gather.4.cloned.1.call-done), kind=kOutput, calls=%fused_computation.104 | convolution fusion | flops 538968064 | bytes 3676160 | tf_op jit(solution)/shard_map/dot_general | solution.py:27
  122.8 5.2 %fusion.27 = bf16[4,256,512]{2,1,0:T(8,128)(2,1)} fusion(bf16[4,256,512]{2,1,0:T(8,128)(2,1)} %get-tuple-element.194, f32[4,256,512]{2,1,0:T(8,128)} %fusion.52, f32[4,256,512]{2,1,0:T(8,128)} %fusion.54, f32[4,256]{1,0:T(4,128)S(1)} %add_rsqrt_fusion.2, f32[512]{0:T(512)S(1)} %bitcast.185, bf16[4,3,512,512]{3,2,1,0:T(8,128)(2,1)} %all-gather.4.cloned.1.call-done, ...), kind=kOutput, calls=%fused_computation.65 | convolution fusion | flops 1081081856 | bytes 8394752 | tf_op jit(solution)/shard_map/dot_general | solution.py:33
  131.0 3.2 %fusion.104 = f32[4,256,512]{2,1,0:T(8,128)} fusion(f32[512]{0:T(512)S(1)} %bitcast.192, f32[4,256]{1,0:T(4,128)S(1)} %add_rsqrt_fusion.7, bf16[4,3,512,512]{3,2,1,0:T(8,128)(2,1)} %all-gather.4.cloned.1.call-done, bf16[4,256,512]{2,1,0:T(8,128)(2,1)S(1)} %gather_fusion, pred[4]{0:T(512)(128)(4,1)S(1)} %get-tuple-element.210), kind=kOutput, calls=%fused_computation.135 | convolution fusion | flops 539492352 | bytes 3676164 | tf_op jit(solution)/shard_map/dot_general | solution.py:27
  137.3 4.6 %fusion.16 = (f32[4,256]{1,0:T(4,128)S(1)}, bf16[4,256,512]{2,1,0:T(8,128)(2,1)}) fusion(bf16[4,512,512]{2,1,0:T(8,128)(2,1)} %all-gather.6.cloned.1.call-done, f32[4,256,512]{2,1,0:T(8,128)} %fusion.104, f32[4,256,512]{2,1,0:T(8,128)} %fusion.106, f32[512]{0:T(512)S(1)} %bitcast.194, f32[4,256]{1,0:T(4,128)S(1)} %add_rsqrt_fusion.7, ...), kind=kOutput, calls=%fused_computation.54 | convolution fusion | flops 1083702272 | bytes 8399872 | tf_op jit(solution)/shard_map/dot_general | solution.py:33
  141.9 3.6 %fusion.82 = f32[4,256,512]{2,1,0:T(8,128)} fusion(bf16[4,256,512]{2,1,0:T(8,128)(2,1)} %get-tuple-element.196, f32[512]{0:T(512)S(1)} %bitcast.186, f32[4,256]{1,0:T(4,128)S(1)} %add_rsqrt_fusion.6, bf16[4,3,512,512]{3,2,1,0:T(8,128)(2,1)} %all-gather.4.cloned.1.call-done), kind=kOutput, calls=%fused_computation.119 | convolution fusion | flops 538968064 | bytes 3676160 | tf_op jit(solution)/shard_map/dot_general | solution.py:27
  148.7 4.3 %fusion.19 = bf16[4,256,512]{2,1,0:T(8,128)(2,1)S(1)} fusion(bf16[4,256,512]{2,1,0:T(8,128)(2,1)} %get-tuple-element.196, f32[4,256,512]{2,1,0:T(8,128)} %fusion.82, f32[4,256,512]{2,1,0:T(8,128)} %fusion.84, f32[512]{0:T(512)S(1)} %bitcast.188, f32[4,256]{1,0:T(4,128)S(1)} %add_rsqrt_fusion.6, bf16[4,3,512,512]{3,2,1,0:T(8,128)(2,1)} %all-gather.4.cloned.1.call-done, ...), kind=kOutput, calls=%fused_computation.57 | convolution fusion | flops 1081081856 | bytes 8394752 | tf_op jit(solution)/shard_map/dot_general | solution.py:33
  156.3 6.6 %all-reduce.18 = (f32[8,18]{1,0:T(8,128)S(1)}, f32[8]{0:T(128)S(1)}) all-reduce(f32[8,18]{1,0:T(8,128)S(1)} %scatter-add.19, f32[8]{0:T(128)S(1)} %fusion.155), channel_id=1, replica_groups=mesh['section'=4,'dp_0'=4,'dp_1'=4,'dp_2'=2] {'section'}, use_global_device_ids=true, to_apply=%region_21.23 | all-reduce | flops 152 | bytes 1216 | tf_op jit(solution)/shard_map/psum | solution.py:16
  163.0 8.6 %all-reduce.17 = (f32[8,18]{1,0:T(8,128)S(1)}, f32[8]{0:T(128)S(1)}) all-reduce(f32[8,18]{1,0:T(8,128)S(1)} %get-tuple-element.167, f32[8]{0:T(128)S(1)} %get-tuple-element.168), channel_id=1, replica_groups=mesh['section'=4,'dp_0'=4,'dp_1'=4,'dp_2'=2] {'dp_0'}, use_global_device_ids=true, to_apply=%region_22.24 | all-reduce | flops 152 | bytes 1216 | tf_op jit(solution)/shard_map/psum | solution.py:16
  171.5 8.7 %all-reduce.16 = (f32[8,18]{1,0:T(8,128)S(1)}, f32[8]{0:T(128)S(1)}) all-reduce(f32[8,18]{1,0:T(8,128)S(1)} %get-tuple-element.165, f32[8]{0:T(128)S(1)} %get-tuple-element.166), channel_id=1, replica_groups=mesh['section'=4,'dp_0'=4,'dp_1'=4,'dp_2'=2] {'dp_1'}, use_global_device_ids=true, to_apply=%region_23.25 | all-reduce | flops 152 | bytes 1216 | tf_op jit(solution)/shard_map/psum | solution.py:16
  180.3 9.1 %all-reduce.19 = (f32[8,18]{1,0:T(8,128)S(1)}, f32[8]{0:T(128)S(1)}) all-reduce(f32[8,18]{1,0:T(8,128)S(1)} %get-tuple-element.163, f32[8]{0:T(128)S(1)} %get-tuple-element.164), channel_id=1, replica_groups=mesh['section'=4,'dp_0'=4,'dp_1'=4,'dp_2'=2] {'dp_2'}, use_global_device_ids=true, to_apply=%region_24.26 | all-reduce | flops 152 | bytes 1216 | tf_op jit(solution)/shard_map/psum | solution.py:16
  203.8 5.2 %fusion.28 = (f32[4,256]{1,0:T(4,128)S(1)}, bf16[4,256,512]{2,1,0:T(8,128)(2,1)}) fusion(f32[4,256,512]{2,1,0:T(8,128)} %bitcast.174, bf16[4,512,512]{2,1,0:T(8,128)(2,1)} %all-gather.6.cloned.1.call-done, f32[4,256,512]{2,1,0:T(8,128)} %fusion.120, f32[4,256,512]{2,1,0:T(8,128)} %fusion.118, bf16[4,256,512]{2,1,0:T(8,128)(2,1)S(1)} %bitcast.172, ...), kind=kOutput, calls=%fused_computation.66 | convolution fusion | flops 1080032256 | bytes 9441280 | tf_op jit(solution)/shard_map/dot_general | solution.py:33
  209.0 3.5 %fusion.48 = f32[4,256,512]{2,1,0:T(8,128)} fusion(bf16[4,256,512]{2,1,0:T(8,128)(2,1)} %get-tuple-element.202, f32[4,256]{1,0:T(4,128)S(1)} %add_rsqrt_fusion, f32[512]{0:T(512)S(1)} %bitcast.177, bf16[4,3,512,512]{3,2,1,0:T(8,128)(2,1)} %all-gather.4.cloned.1.call-done), kind=kOutput, calls=%fused_computation.103 | convolution fusion | flops 538968064 | bytes 3676160 | tf_op jit(solution)/shard_map/dot_general | solution.py:27
  215.7 3.8 %fusion.43 = f32[4,256]{1,0:T(4,128)S(1)} fusion(f32[4,256,512]{2,1,0:T(8,128)} %fusion.46, f32[4,256,512]{2,1,0:T(8,128)} %fusion.48, bf16[4,256,512]{2,1,0:T(8,128)(2,1)S(1)} %copy-done.14, f32[4,256]{1,0:T(4,128)S(1)} %add_rsqrt_fusion, f32[512]{0:T(512)S(1)} %bitcast.179, bf16[4,3,512,512]{3,2,1,0:T(8,128)(2,1)} %all-gather.4.cloned.1.call-done, ...), kind=kOutput, calls=%fused_computation.81 | convolution fusion | flops 1084226560 | bytes 8399360 | tf_op jit(solution)/shard_map/dot_general | solution.py:33
  222.5 3.3 %fusion.119 = f32[4,256,512]{2,1,0:T(8,128)} fusion(bf16[4,256,512]{2,1,0:T(8,128)(2,1)S(1)} %bitcast.168, bf16[4,3,512,512]{3,2,1,0:T(8,128)(2,1)} %all-gather.4.cloned.1.call-done), kind=kOutput, calls=%fused_computation.159 | convolution fusion | flops 536870912 | bytes 3670016 | tf_op jit(solution)/shard_map/dot_general | solution.py:27
  225.8 4.4 %fusion.20 = (f32[4,256]{1,0:T(4,128)S(1)}, bf16[4,256,512]{2,1,0:T(8,128)(2,1)}) fusion(f32[4,256,512]{2,1,0:T(8,128)S(1)} %bitcast.173, bf16[4,512,512]{2,1,0:T(8,128)(2,1)} %all-gather.6.cloned.1.call-done, f32[4,256,512]{2,1,0:T(8,128)} %fusion.121, f32[4,256,512]{2,1,0:T(8,128)} %fusion.119, bf16[4,256,512]{2,1,0:T(8,128)(2,1)S(1)} %bitcast.169, ...), kind=kOutput, calls=%fused_computation.58 | convolution fusion | flops 1080032256 | bytes 9441280 | tf_op jit(solution)/shard_map/dot_general | solution.py:33
  230.2 3.6 %fusion.68 = f32[4,256,512]{2,1,0:T(8,128)} fusion(bf16[4,256,512]{2,1,0:T(8,128)(2,1)} %get-tuple-element.204, f32[512]{0:T(512)S(1)} %bitcast.180, f32[4,256]{1,0:T(4,128)S(1)} %add_rsqrt_fusion.4, bf16[4,3,512,512]{3,2,1,0:T(8,128)(2,1)} %all-gather.4.cloned.1.call-done), kind=kOutput, calls=%fused_computation.111 | convolution fusion | flops 538968064 | bytes 3676160 | tf_op jit(solution)/shard_map/dot_general | solution.py:27
  237.0 3.8 %fusion.37 = f32[4,256]{1,0:T(4,128)S(1)} fusion(f32[4,256,512]{2,1,0:T(8,128)} %fusion.68, f32[4,256,512]{2,1,0:T(8,128)} %fusion.70, bf16[4,256,512]{2,1,0:T(8,128)(2,1)S(1)} %copy-done.13, f32[512]{0:T(512)S(1)} %bitcast.182, f32[4,256]{1,0:T(4,128)S(1)} %add_rsqrt_fusion.4, bf16[4,3,512,512]{3,2,1,0:T(8,128)(2,1)} %all-gather.4.cloned.1.call-done, ...), kind=kOutput, calls=%fused_computation.75 | convolution fusion | flops 1084226560 | bytes 8399360 | tf_op jit(solution)/shard_map/dot_general | solution.py:33
  (102 shorter events, 47.6 us)
Async XLA Ops:
  7.2 187.9 %copy-start = (bf16[18,512]{1,0:T(8,128)(2,1)S(1)}, bf16[18,512]{1,0:T(8,128)(2,1)}, u32[]{:S(2)}) copy-start(bf16[18,512]{1,0:T(8,128)(2,1)} %param.43) | copy-start | bytes 55300
  7.2 1.5 copy-start.7
  7.2 12.6 %copy-start.8 = (s32[8,4]{0,1:T(4,128)S(1)}, s32[8,4]{0,1:T(4,128)}, u32[]{:S(2)}) copy-start(s32[8,4]{0,1:T(4,128)} %param.36) | copy-start | bytes 388
  7.2 71.3 %all-gather.4.cloned.1.call-start = ((), (), s32[]{:S(2)}) async-start(), calls=%async_computation | async-start | bytes 7864320 | tf_op jit(solution)/shard_map/all_gather | solution.py:97
  7.9 103.5 %all-gather.6.cloned.1.call-start = ((), (), s32[]{:S(2)}) async-start(), calls=%async_computation.1 | async-start | bytes 2621440 | tf_op jit(solution)/shard_map/all_gather | solution.py:98
  20.1 14.8 %copy-start.10 = (bf16[1,512]{1,0:T(2,128)(2,1)S(1)}, bf16[1,512]{1,0:T(2,128)(2,1)}, u32[]{:S(2)}) copy-start(bf16[1,512]{1,0:T(2,128)(2,1)} %param.40) | copy-start | bytes 3076
  20.1 25.6 %copy-start.9 = (s32[2]{0:T(128)S(1)}, s32[2]{0:T(128)}, u32[]{:S(2)}) copy-start(s32[2]{0:T(128)} %constant.322.clone.1) | copy-start | bytes 28
  24.8 112.5 %copy-start.5 = (bf16[4,256,512]{2,1,0:T(8,128)(2,1)}, bf16[4,256,512]{2,1,0:T(8,128)(2,1)S(1)}, u32[]{:S(2)}) copy-start(bf16[4,256,512]{2,1,0:T(8,128)(2,1)S(1)} %gather_fusion) | copy-start | bytes 3145732
  116.1 3.5 %copy-start.16 = (bf16[4,256,512]{2,1,0:T(8,128)(2,1)S(1)}, bf16[4,256,512]{2,1,0:T(8,128)(2,1)}, u32[]{:S(2)}) copy-start(bf16[4,256,512]{2,1,0:T(8,128)(2,1)} %get-tuple-element.194) | copy-start | bytes 3145732
  122.8 5.2 %copy-start.11 = (bf16[512,18]{0,1:T(8,128)(2,1)S(1)}, bf16[512,18]{0,1:T(8,128)(2,1)}, u32[]{:S(2)}) copy-start(bf16[512,18]{0,1:T(8,128)(2,1)} %param.41) | copy-start | bytes 55300
  122.8 5.2 %copy-start.12 = (f32[18]{0:T(128)S(1)}, f32[18]{0:T(128)}, u32[]{:S(2)}) copy-start(f32[18]{0:T(128)} %param.42) | copy-start | bytes 220
  141.9 3.6 %copy-start.15 = (bf16[4,256,512]{2,1,0:T(8,128)(2,1)S(1)}, bf16[4,256,512]{2,1,0:T(8,128)(2,1)}, u32[]{:S(2)}) copy-start(bf16[4,256,512]{2,1,0:T(8,128)(2,1)} %get-tuple-element.196) | copy-start | bytes 3145732
  195.7 1.4 copy-start.2
  196.2 1.4 copy-start.4
  209.0 3.5 %copy-start.14 = (bf16[4,256,512]{2,1,0:T(8,128)(2,1)S(1)}, bf16[4,256,512]{2,1,0:T(8,128)(2,1)}, u32[]{:S(2)}) copy-start(bf16[4,256,512]{2,1,0:T(8,128)(2,1)} %get-tuple-element.202) | copy-start | bytes 3145732
  222.5 3.3 %copy-start.3 = (f32[1024,512]{1,0:T(8,128)S(1)}, f32[1024,512]{1,0:T(8,128)}, u32[]{:S(2)}) copy-start(f32[1024,512]{1,0:T(8,128)} %copy-done.2) | copy-start | bytes 6291460
  230.2 3.6 %copy-start.13 = (bf16[4,256,512]{2,1,0:T(8,128)(2,1)S(1)}, bf16[4,256,512]{2,1,0:T(8,128)(2,1)}, u32[]{:S(2)}) copy-start(bf16[4,256,512]{2,1,0:T(8,128)(2,1)} %get-tuple-element.204) | copy-start | bytes 3145732
  233.8 3.2 %copy-start.6 = (bf16[4,256,512]{2,1,0:T(8,128)(2,1)S(1)}, bf16[4,256,512]{2,1,0:T(8,128)(2,1)}, u32[]{:S(2)}) copy-start(bf16[4,256,512]{2,1,0:T(8,128)(2,1)} %copy-done.5) | copy-start | bytes 3145732
  237.0 4.9 %copy-start.1 = (bf16[18,512]{1,0:T(8,128)(2,1)S(1)}, bf16[18,512]{1,0:T(8,128)(2,1)}, u32[]{:S(2)}) copy-start(bf16[18,512]{1,0:T(8,128)(2,1)} %param.43) | copy-start | bytes 55300
Sparse Core Ops, SparseCore 0:
  9.7 68.7 all-gather.3
  80.1 31.2 all-gather.5
where the time goes:
time: 250 us; the launch traced here: 249 us
  matrix products  92.5 us (37%)
  waiting for transfers between devices  58.3 us (23%)
  blocking collectives  43.8 us (18%)
  between operations  31.2 us (12%)
  local copies, waits for them, and re-layouts  11.8 us (5%)
  other arithmetic  11.1 us (4%)
    dot_general x16, matrix products, run_block(): jnp.dot(flat, tap_set[k], preferred_element_type=jnp.float32)  52 us
    dot_general x8, matrix products, run_block(): jnp.dot(activated.reshape(-1, channels), out_weight, preferred_element_ty...  35.9 us
    psum x4, blocking collectives, over_axes(): return functools.reduce(lax.psum, axes, array)  33 us
    all_gather x1, waiting for transfers between devices, on_device(): lax.all_gather(tap_weights, 'section', axis=0, tiled=True)  30.2 us
    all_gather x1, waiting for transfers between devices, on_device(): lax.all_gather(out_weights, 'section', axis=0, tiled=True)  26.6 us
    all_gather x1, blocking collectives, on_device(): lax.all_gather(norm_gains, 'section', axis=0, tiled=True)  10.8 us
    gather x2, local copies, waits for them, and re-layouts, on_device(): source = jnp.take(clip_pool, clip_index[batch_slot], axis=0)  9.48 us
    another operation x12, other arithmetic  8.18 us
  transfers between devices with their start and end apart: 2, of which 2 were waited for; matrix products, arithmetic and copies ran while one was open for 8% of the time, Pallas kernels for 0%

commit v1 on v0

--- a/solution.py
+++ b/solution.py
@@ -93,8 +93,16 @@
     rows_total = float(clip_count * lax.axis_size(DP) * row_count)
     bit_buffer = jnp.zeros((batches, quant_weight.shape[1]), jnp.float32)
     entropy_buffer = jnp.zeros((batches,), jnp.float32)
+
+    def deliver_lots_all_now(state):
+        cores_n = lax.psum(1, "section")
+        pieces_in = tuple((cores_n if at == 0 else 1 for at in range(state.ndim)))
+        return lax.all_to_all(
+            jnp.tile(state, pieces_in), "section", split_axis=0, concat_axis=0, tiled=True
+        )
+
     all_taps, all_out, all_gains = (
-        lax.all_gather(tap_weights, "section", axis=0, tiled=True),
+        deliver_lots_all_now(tap_weights),
         lax.all_gather(out_weights, "section", axis=0, tiled=True),
         lax.all_gather(norm_gains, "section", axis=0, tiled=True),
     )

time: 250 us -> 261 us (1.044)
  blocking collectives: 43.8 us -> 103 us
  waiting for transfers between devices: 58.3 us -> 0.68 us
  starting transfers between devices: 0.08 us -> 5.41 us
  local copies, waits for them, and re-layouts: 11.8 us -> 15.5 us
    all_gather x1, blocking collectives: 10.8 us -> 65.1 us  [on_device(): lax.all_gather(norm_gains, 'section', axis=0, tiled=True)]
    all_gather x1 -> x0, waiting for transfers between devices: 30.2 us -> none  [on_device(): lax.all_gather(tap_weights, 'section', axis=0, tiled=True)]
    all_gather x1, waiting for transfers between devices: 26.6 us -> 0.01 us  [on_device(): lax.all_gather(out_weights, 'section', axis=0, tiled=True)]
    all_to_all x0 -> x1, starting transfers between devices: none -> 5.37 us  [deliver_lots_all_now(): lax.all_to_all(jnp.tile(state, pieces_in), 'section', split_axis=0, conca...]
    another operation x3 -> x4, local copies, waits for them, and re-layouts: 0.01 us -> 4.62 us  [the longest x1 4.61 us: deliver_lots_all_now(): jnp.tile(state, pieces_in)]
    psum x4, blocking collectives: 33 us -> 37.6 us  [over_axes(): return functools.reduce(lax.psum, axes, array)]
  transfers between devices with their start and end apart: 2 -> 2, of which waited for: 2 -> 0; matrix products, arithmetic and copies ran while one was open for 8% -> 7% of each run, Pallas kernels for 0% -> 0%
where the time goes in v1:
time: 261 us; the launch traced here: 259 us
  blocking collectives  103 us (39%)
  matrix products  92.6 us (35%)
  between operations  31.1 us (12%)
  local copies, waits for them, and re-layouts  15.5 us (6%)
  other arithmetic  11.1 us (4%)
  starting transfers between devices  5.41 us (2%)
    all_gather x1, blocking collectives, on_device(): lax.all_gather(norm_gains, 'section', axis=0, tiled=True)  65.1 us
    dot_general x16, matrix products, run_block(): jnp.dot(flat, tap_set[k], preferred_element_type=jnp.float32)  52.3 us
    psum x4, blocking collectives, over_axes(): return functools.reduce(lax.psum, axes, array)  37.6 us
    dot_general x8, matrix products, run_block(): jnp.dot(activated.reshape(-1, channels), out_weight, preferred_element_ty...  35.7 us
    gather x2, local copies, waits for them, and re-layouts, on_device(): source = jnp.take(clip_pool, clip_index[batch_slot], axis=0)  8.58 us
    another operation x12, other arithmetic  8.18 us
    all_to_all x1, starting transfers between devices, deliver_lots_all_now(): lax.all_to_all(jnp.tile(state, pieces_in), 'section', split_axis=0, conca...  5.37 us
  transfers between devices with their start and end apart: 2, of which 0 were waited for; matrix products, arithmetic and copies ran while one was open for 7% of the time, Pallas kernels for 0%

profile of v1, /device:TPU:1, one launch (start us, length us, event | category | flops | bytes accessed | tf_op | source)
XLA Modules:
  0.0 259.1 jit_solution(2954076883967541740)
XLA Ops:
  7.2 4.6 %tile.10 = bf16[4,3,512,512]{3,2,1,0:T(8,128)(2,1)} broadcast(bf16[3,512,512]{2,1,0:T(8,128)(2,1)} %bitcast.176), dimensions={1,2,3} | broadcast | bytes 7864320 | tf_op jit(solution)/shard_map/tile | solution.py:101
  11.8 5.4 %all-to-all-start = ((bf16[4,3,512,512]{3,2,1,0:T(8,128)(2,1)}), bf16[4,3,512,512]{3,2,1,0:T(8,128)(2,1)}, u32[]{:S(2)}, u32[]{:S(2)}) async-start(bf16[4,3,512,512]{3,2,1,0:T(8,128)(2,1)} %tile.10), calls=%async_computation | async-start | bytes 12582912 | tf_op jit(solution)/shard_map/all_to_all | solution.py:100
  29.2 4.1 %gather_fusion = bf16[4,256,512]{2,1,0:T(8,128)(2,1)S(1)} fusion(bf16[32,256,512]{2,1,0:T(8,128)(2,1)} %param.35, s32[1024]{0:T(1024)S(1)} %pad_clamp_fusion.1), kind=kCustom, calls=%fused_computation.clone | custom fusion | bytes 2097168 | tf_op jit(solution)/shard_map/jit(_take)/gather | solution.py:113
  33.3 4.5 %gather_fusion.1 = bf16[4,256,512]{2,1,0:T(8,128)(2,1)S(1)} fusion(bf16[32,256,512]{2,1,0:T(8,128)(2,1)} %param.35, s32[1024]{0:T(1024)S(1)} %pad_clamp_fusion), kind=kCustom, calls=%fused_computation.1.clone | custom fusion | bytes 2097168 | tf_op jit(solution)/shard_map/jit(_take)/gather | solution.py:113
  43.0 65.1 %all-gather = bf16[4,1,512]{2,1,0:T(2,128)(2,1)S(1)} all-gather(bf16[1,1,512]{2,1,0:T(2,128)(2,1)S(1)} %bitcast.178), channel_id=1, replica_groups=mesh['section'=4,'dp_0'=4,'dp_1'=4,'dp_2'=2] {'section'}, dimensions={0}, use_global_device_ids=true | all-gather | bytes 5120 | tf_op jit(solution)/shard_map/all_gather | solution.py:107
  113.8 3.2 %fusion.60 = f32[4,256,512]{2,1,0:T(8,128)} fusion(f32[4,256]{1,0:T(4,128)S(1)} %add_rsqrt_fusion.3, f32[512]{0:T(512)S(1)} %bitcast.192, bf16[4,3,512,512]{3,2,1,0:T(8,128)(2,1)} %all-to-all-done, bf16[4,256,512]{2,1,0:T(8,128)(2,1)S(1)} %gather_fusion.1, pred[4]{0:T(512)(128)(4,1)S(1)} %get-tuple-element.209), kind=kOutput, calls=%fused_computation.107 | convolution fusion | flops 539492352 | bytes 3676164 | tf_op jit(solution)/shard_map/dot_general | solution.py:27
  117.0 4.5 %fusion.24 = (f32[4,256]{1,0:T(4,128)S(1)}, bf16[4,256,512]{2,1,0:T(8,128)(2,1)}) fusion(bf16[4,512,512]{2,1,0:T(8,128)(2,1)} %all-gather.3.cloned.1.call-done, f32[4,256,512]{2,1,0:T(8,128)} %fusion.58, f32[4,256,512]{2,1,0:T(8,128)} %fusion.60, f32[4,256]{1,0:T(4,128)S(1)} %add_rsqrt_fusion.3, f32[512]{0:T(512)S(1)} %bitcast.193, ...), kind=kOutput, calls=%fused_computation.62 | convolution fusion | flops 1083702272 | bytes 8399872 | tf_op jit(solution)/shard_map/dot_general | solution.py:33
  121.6 3.6 %fusion.54 = f32[4,256,512]{2,1,0:T(8,128)} fusion(bf16[4,256,512]{2,1,0:T(8,128)(2,1)} %get-tuple-element.194, f32[4,256]{1,0:T(4,128)S(1)} %add_rsqrt_fusion.2, f32[512]{0:T(512)S(1)} %bitcast.185, bf16[4,3,512,512]{3,2,1,0:T(8,128)(2,1)} %all-to-all-done), kind=kOutput, calls=%fused_computation.105 | convolution fusion | flops 538968064 | bytes 3676160 | tf_op jit(solution)/shard_map/dot_general | solution.py:27
  128.4 5.2 %fusion.27 = bf16[4,256,512]{2,1,0:T(8,128)(2,1)} fusion(bf16[4,256,512]{2,1,0:T(8,128)(2,1)} %get-tuple-element.194, f32[4,256,512]{2,1,0:T(8,128)} %fusion.52, f32[4,256,512]{2,1,0:T(8,128)} %fusion.54, f32[4,256]{1,0:T(4,128)S(1)} %add_rsqrt_fusion.2, f32[512]{0:T(512)S(1)} %bitcast.187, bf16[4,3,512,512]{3,2,1,0:T(8,128)(2,1)} %all-to-all-done, ...), kind=kOutput, calls=%fused_computation.65 | convolution fusion | flops 1081081856 | bytes 8394752 | tf_op jit(solution)/shard_map/dot_general | solution.py:33
  139.7 3.2 %fusion.106 = f32[4,256,512]{2,1,0:T(8,128)} fusion(f32[512]{0:T(512)S(1)} %bitcast.195, f32[4,256]{1,0:T(4,128)S(1)} %add_rsqrt_fusion.7, bf16[4,3,512,512]{3,2,1,0:T(8,128)(2,1)} %all-to-all-done, bf16[4,256,512]{2,1,0:T(8,128)(2,1)S(1)} %gather_fusion, pred[4]{0:T(512)(128)(4,1)S(1)} %get-tuple-element.210), kind=kOutput, calls=%fused_computation.136 | convolution fusion | flops 539492352 | bytes 3676164 | tf_op jit(solution)/shard_map/dot_general | solution.py:27
  142.9 4.5 %fusion.16 = (f32[4,256]{1,0:T(4,128)S(1)}, bf16[4,256,512]{2,1,0:T(8,128)(2,1)}) fusion(bf16[4,512,512]{2,1,0:T(8,128)(2,1)} %all-gather.3.cloned.1.call-done, f32[4,256,512]{2,1,0:T(8,128)} %fusion.104, f32[4,256,512]{2,1,0:T(8,128)} %fusion.106, f32[512]{0:T(512)S(1)} %bitcast.196, f32[4,256]{1,0:T(4,128)S(1)} %add_rsqrt_fusion.7, ...), kind=kOutput, calls=%fused_computation.54 | convolution fusion | flops 1083702272 | bytes 8399872 | tf_op jit(solution)/shard_map/dot_general | solution.py:33
  147.5 3.5 %fusion.82 = f32[4,256,512]{2,1,0:T(8,128)} fusion(bf16[4,256,512]{2,1,0:T(8,128)(2,1)} %get-tuple-element.196, f32[512]{0:T(512)S(1)} %bitcast.188, f32[4,256]{1,0:T(4,128)S(1)} %add_rsqrt_fusion.6, bf16[4,3,512,512]{3,2,1,0:T(8,128)(2,1)} %all-to-all-done), kind=kOutput, calls=%fused_computation.119 | convolution fusion | flops 538968064 | bytes 3676160 | tf_op jit(solution)/shard_map/dot_general | solution.py:27
  154.2 4.3 %fusion.19 = bf16[4,256,512]{2,1,0:T(8,128)(2,1)S(1)} fusion(bf16[4,256,512]{2,1,0:T(8,128)(2,1)} %get-tuple-element.196, f32[4,256,512]{2,1,0:T(8,128)} %fusion.82, f32[4,256,512]{2,1,0:T(8,128)} %fusion.84, f32[512]{0:T(512)S(1)} %bitcast.190, f32[4,256]{1,0:T(4,128)S(1)} %add_rsqrt_fusion.6, bf16[4,3,512,512]{3,2,1,0:T(8,128)(2,1)} %all-to-all-done, ...), kind=kOutput, calls=%fused_computation.57 | convolution fusion | flops 1081081856 | bytes 8394752 | tf_op jit(solution)/shard_map/dot_general | solution.py:33
  162.0 7.3 %all-reduce.18 = (f32[8,18]{1,0:T(8,128)S(1)}, f32[8]{0:T(128)S(1)}) all-reduce(f32[8,18]{1,0:T(8,128)S(1)} %scatter-add.19, f32[8]{0:T(128)S(1)} %fusion.155), channel_id=1, replica_groups=mesh['section'=4,'dp_0'=4,'dp_1'=4,'dp_2'=2] {'section'}, use_global_device_ids=true, to_apply=%region_21.23 | all-reduce | flops 152 | bytes 1216 | tf_op jit(solution)/shard_map/psum | solution.py:16
  169.3 9.2 %all-reduce.17 = (f32[8,18]{1,0:T(8,128)S(1)}, f32[8]{0:T(128)S(1)}) all-reduce(f32[8,18]{1,0:T(8,128)S(1)} %get-tuple-element.167, f32[8]{0:T(128)S(1)} %get-tuple-element.168), channel_id=1, replica_groups=mesh['section'=4,'dp_0'=4,'dp_1'=4,'dp_2'=2] {'dp_0'}, use_global_device_ids=true, to_apply=%region_22.24 | all-reduce | flops 152 | bytes 1216 | tf_op jit(solution)/shard_map/psum | solution.py:16
  178.5 9.8 %all-reduce.16 = (f32[8,18]{1,0:T(8,128)S(1)}, f32[8]{0:T(128)S(1)}) all-reduce(f32[8,18]{1,0:T(8,128)S(1)} %get-tuple-element.165, f32[8]{0:T(128)S(1)} %get-tuple-element.166), channel_id=1, replica_groups=mesh['section'=4,'dp_0'=4,'dp_1'=4,'dp_2'=2] {'dp_1'}, use_global_device_ids=true, to_apply=%region_23.25 | all-reduce | flops 152 | bytes 1216 | tf_op jit(solution)/shard_map/psum | solution.py:16
  188.4 11.2 %all-reduce.19 = (f32[8,18]{1,0:T(8,128)S(1)}, f32[8]{0:T(128)S(1)}) all-reduce(f32[8,18]{1,0:T(8,128)S(1)} %get-tuple-element.163, f32[8]{0:T(128)S(1)} %get-tuple-element.164), channel_id=1, replica_groups=mesh['section'=4,'dp_0'=4,'dp_1'=4,'dp_2'=2] {'dp_2'}, use_global_device_ids=true, to_apply=%region_24.26 | all-reduce | flops 152 | bytes 1216 | tf_op jit(solution)/shard_map/psum | solution.py:16
  214.1 5.2 %fusion.28 = (f32[4,256]{1,0:T(4,128)S(1)}, bf16[4,256,512]{2,1,0:T(8,128)(2,1)}) fusion(f32[4,256,512]{2,1,0:T(8,128)} %bitcast.175, bf16[4,512,512]{2,1,0:T(8,128)(2,1)} %all-gather.3.cloned.1.call-done, f32[4,256,512]{2,1,0:T(8,128)} %fusion.120, f32[4,256,512]{2,1,0:T(8,128)} %fusion.118, bf16[4,256,512]{2,1,0:T(8,128)(2,1)S(1)} %bitcast.173, ...), kind=kOutput, calls=%fused_computation.66 | convolution fusion | flops 1080032256 | bytes 9441280 | tf_op jit(solution)/shard_map/dot_general | solution.py:33
  219.3 3.6 %fusion.48 = f32[4,256,512]{2,1,0:T(8,128)} fusion(bf16[4,256,512]{2,1,0:T(8,128)(2,1)} %get-tuple-element.202, f32[4,256]{1,0:T(4,128)S(1)} %add_rsqrt_fusion, f32[512]{0:T(512)S(1)} %bitcast.179, bf16[4,3,512,512]{3,2,1,0:T(8,128)(2,1)} %all-to-all-done), kind=kOutput, calls=%fused_computation.103 | convolution fusion | flops 538968064 | bytes 3676160 | tf_op jit(solution)/shard_map/dot_general | solution.py:27
  226.0 3.8 %fusion.43 = f32[4,256]{1,0:T(4,128)S(1)} fusion(f32[4,256,512]{2,1,0:T(8,128)} %fusion.46, f32[4,256,512]{2,1,0:T(8,128)} %fusion.48, bf16[4,256,512]{2,1,0:T(8,128)(2,1)S(1)} %copy-done.14, f32[4,256]{1,0:T(4,128)S(1)} %add_rsqrt_fusion, f32[512]{0:T(512)S(1)} %bitcast.181, bf16[4,3,512,512]{3,2,1,0:T(8,128)(2,1)} %all-to-all-done, ...), kind=kOutput, calls=%fused_computation.81 | convolution fusion | flops 1084226560 | bytes 8399360 | tf_op jit(solution)/shard_map/dot_general | solution.py:33
  236.1 4.4 %fusion.20 = (f32[4,256]{1,0:T(4,128)S(1)}, bf16[4,256,512]{2,1,0:T(8,128)(2,1)}) fusion(f32[4,256,512]{2,1,0:T(8,128)S(1)} %bitcast.174, bf16[4,512,512]{2,1,0:T(8,128)(2,1)} %all-gather.3.cloned.1.call-done, f32[4,256,512]{2,1,0:T(8,128)} %fusion.121, f32[4,256,512]{2,1,0:T(8,128)} %fusion.119, bf16[4,256,512]{2,1,0:T(8,128)(2,1)S(1)} %bitcast.170, ...), kind=kOutput, calls=%fused_computation.58 | convolution fusion | flops 1080032256 | bytes 9441280 | tf_op jit(solution)/shard_map/dot_general | solution.py:33
  240.5 3.6 %fusion.68 = f32[4,256,512]{2,1,0:T(8,128)} fusion(bf16[4,256,512]{2,1,0:T(8,128)(2,1)} %get-tuple-element.204, f32[512]{0:T(512)S(1)} %bitcast.182, f32[4,256]{1,0:T(4,128)S(1)} %add_rsqrt_fusion.4, bf16[4,3,512,512]{3,2,1,0:T(8,128)(2,1)} %all-to-all-done), kind=kOutput, calls=%fused_computation.111 | convolution fusion | flops 538968064 | bytes 3676160 | tf_op jit(solution)/shard_map/dot_general | solution.py:27
  244.1 3.3 %fusion.70 = f32[4,256,512]{2,1,0:T(8,128)} fusion(bf16[4,256,512]{2,1,0:T(8,128)(2,1)S(1)} %copy-done.13, f32[512]{0:T(512)S(1)} %bitcast.183, f32[4,256]{1,0:T(4,128)S(1)} %add_rsqrt_fusion.4, bf16[4,3,512,512]{3,2,1,0:T(8,128)(2,1)} %all-to-all-done), kind=kOutput, calls=%fused_computation.112 | convolution fusion | flops 538968064 | bytes 3676160 | tf_op jit(solution)/shard_map/dot_general | solution.py:27
  247.4 3.7 %fusion.37 = f32[4,256]{1,0:T(4,128)S(1)} fusion(f32[4,256,512]{2,1,0:T(8,128)} %fusion.68, f32[4,256,512]{2,1,0:T(8,128)} %fusion.70, bf16[4,256,512]{2,1,0:T(8,128)(2,1)S(1)} %copy-done.13, f32[512]{0:T(512)S(1)} %bitcast.184, f32[4,256]{1,0:T(4,128)S(1)} %add_rsqrt_fusion.4, bf16[4,3,512,512]{3,2,1,0:T(8,128)(2,1)} %all-to-all-done, ...), kind=kOutput, calls=%fused_computation.75 | convolution fusion | flops 1084226560 | bytes 8399360 | tf_op jit(solution)/shard_map/dot_general | solution.py:33
  (102 shorter events, 47.0 us)
Async XLA Ops:
  7.2 198.2 %copy-start = (bf16[18,512]{1,0:T(8,128)(2,1)S(1)}, bf16[18,512]{1,0:T(8,128)(2,1)}, u32[]{:S(2)}) copy-start(bf16[18,512]{1,0:T(8,128)(2,1)} %param.43) | copy-start | bytes 55300
  11.8 6.1 %copy-start.7 = (s32[8]{0:T(128)S(1)}, s32[8]{0:T(128)}, u32[]{:S(2)}) copy-start(s32[8]{0:T(128)} %param.37) | copy-start | bytes 100
  11.8 17.1 %copy-start.8 = (s32[8,4]{0,1:T(4,128)S(1)}, s32[8,4]{0,1:T(4,128)}, u32[]{:S(2)}) copy-start(s32[8,4]{0,1:T(4,128)} %param.36) | copy-start | bytes 388
  11.8 98.9 %all-to-all-start = ((bf16[4,3,512,512]{3,2,1,0:T(8,128)(2,1)}), bf16[4,3,512,512]{3,2,1,0:T(8,128)(2,1)}, u32[]{:S(2)}, u32[]{:S(2)}) async-start(bf16[4,3,512,512]{3,2,1,0:T(8,128)(2,1)} %tile.10), calls=%async_computation | async-start | bytes 12582912 | tf_op jit(solution)/shard_map/all_to_all | solution.py:100
  17.2 99.9 %all-gather.3.cloned.1.call-start = ((), (), s32[]{:S(2)}) async-start(), calls=%async_computation.1 | async-start | bytes 2621440 | tf_op jit(solution)/shard_map/all_gather | solution.py:106
  29.2 13.8 %copy-start.10 = (bf16[1,512]{1,0:T(2,128)(2,1)S(1)}, bf16[1,512]{1,0:T(2,128)(2,1)}, u32[]{:S(2)}) copy-start(bf16[1,512]{1,0:T(2,128)(2,1)} %param.40) | copy-start | bytes 3076
  29.2 78.9 %copy-start.9 = (s32[2]{0:T(128)S(1)}, s32[2]{0:T(128)}, u32[]{:S(2)}) copy-start(s32[2]{0:T(128)} %constant.322.clone.1) | copy-start | bytes 28
  33.3 109.6 %copy-start.5 = (bf16[4,256,512]{2,1,0:T(8,128)(2,1)}, bf16[4,256,512]{2,1,0:T(8,128)(2,1)S(1)}, u32[]{:S(2)}) copy-start(bf16[4,256,512]{2,1,0:T(8,128)(2,1)S(1)} %gather_fusion) | copy-start | bytes 3145732
  121.6 3.6 %copy-start.16 = (bf16[4,256,512]{2,1,0:T(8,128)(2,1)S(1)}, bf16[4,256,512]{2,1,0:T(8,128)(2,1)}, u32[]{:S(2)}) copy-start(bf16[4,256,512]{2,1,0:T(8,128)(2,1)} %get-tuple-element.194) | copy-start | bytes 3145732
  128.4 5.2 %copy-start.11 = (bf16[512,18]{0,1:T(8,128)(2,1)S(1)}, bf16[512,18]{0,1:T(8,128)(2,1)}, u32[]{:S(2)}) copy-start(bf16[512,18]{0,1:T(8,128)(2,1)} %param.41) | copy-start | bytes 55300
  128.4 5.2 %copy-start.12 = (f32[18]{0:T(128)S(1)}, f32[18]{0:T(128)}, u32[]{:S(2)}) copy-start(f32[18]{0:T(128)} %param.42) | copy-start | bytes 220
  147.5 3.6 %copy-start.15 = (bf16[4,256,512]{2,1,0:T(8,128)(2,1)S(1)}, bf16[4,256,512]{2,1,0:T(8,128)(2,1)}, u32[]{:S(2)}) copy-start(bf16[4,256,512]{2,1,0:T(8,128)(2,1)} %get-tuple-element.196) | copy-start | bytes 3145732
  205.9 1.3 copy-start.2
  206.5 1.5 copy-start.4
  219.3 3.6 %copy-start.14 = (bf16[4,256,512]{2,1,0:T(8,128)(2,1)S(1)}, bf16[4,256,512]{2,1,0:T(8,128)(2,1)}, u32[]{:S(2)}) copy-start(bf16[4,256,512]{2,1,0:T(8,128)(2,1)} %get-tuple-element.202) | copy-start | bytes 3145732
  232.9 3.2 %copy-start.3 = (f32[1024,512]{1,0:T(8,128)S(1)}, f32[1024,512]{1,0:T(8,128)}, u32[]{:S(2)}) copy-start(f32[1024,512]{1,0:T(8,128)} %copy-done.2) | copy-start | bytes 6291460
  240.5 3.6 %copy-start.13 = (bf16[4,256,512]{2,1,0:T(8,128)(2,1)S(1)}, bf16[4,256,512]{2,1,0:T(8,128)(2,1)}, u32[]{:S(2)}) copy-start(bf16[4,256,512]{2,1,0:T(8,128)(2,1)} %get-tuple-element.204) | copy-start | bytes 3145732
  244.1 3.3 %copy-start.6 = (bf16[4,256,512]{2,1,0:T(8,128)(2,1)S(1)}, bf16[4,256,512]{2,1,0:T(8,128)(2,1)}, u32[]{:S(2)}) copy-start(bf16[4,256,512]{2,1,0:T(8,128)(2,1)} %copy-done.5) | copy-start | bytes 3145732
  247.4 4.9 %copy-start.1 = (bf16[18,512]{1,0:T(8,128)(2,1)S(1)}, bf16[18,512]{1,0:T(8,128)(2,1)}, u32[]{:S(2)}) copy-start(bf16[18,512]{1,0:T(8,128)(2,1)} %param.43) | copy-start | bytes 55300
Sparse Core Ops, SparseCore 0:
  19.7 51.3 all-gather.2
